TPU v7x, 32 devices: a whole 2x2x4 slice. The times are simulated.
32 devices in a mesh: rep: 4 (over y, x), tp: 8 (over z, core).
Axes of the slice: x: 2, y: 2, z: 4, core: 2. Of those that a mesh axis runs over, the one named last changes fastest.
Arguments:
- hidden: bfloat16 [2048, 14336], P('rep'), may hold values from -6 to 6
- ln_gain: float32 [14336], replicated, may hold values from 0.1 to 1.9
- ln_shift: float32 [14336], replicated, may hold values from -3 to 3
- qkv_weight: bfloat16 [14336, 16, 384], P(('rep', 'tp')), may hold values from -0.046875 to 0.046875
- qkv_bias: float32 [16, 384], P('tp'), may hold values from -64 to 64
- out_weight: bfloat16 [14336, 16, 128], P('tp'), may hold values from -0.375 to 0.375
- out_bias: float32 [14336], P('tp'), may hold values from -3 to 3
- slope_index: int32 [16], P('tp'), may hold values from 0 to 111
Outputs:
- attended: bfloat16 [2048, 14336], P('rep', 'tp')
All inputs are finite; a program needn't handle non-finite values.
Results may differ from a plain program's by a relative error of at most 0.024.
The roundings to bfloat16 on the way count: a program that leaves them out, or rounds other values in their place, can miss the bound.
Values may be sent and summed in bfloat16 or wider, within the bound.
A program may use at most 192 MiB of HBM per device.

v0:
```python
import math

import jax
import jax.numpy as jnp
from jax import lax
from jax.sharding import PartitionSpec as P

N_SLOPES = 112


epsilon = 1e-05


def slope_values(slope_index):
    power = 1 << N_SLOPES.bit_length() - 1
    index_float = slope_index.astype(jnp.float32)
    leading = jnp.exp2(-8.0 * (index_float + 1.0) / power)
    between = jnp.exp2(-4.0 * (2.0 * (index_float - power) + 1.0) / power)
    return jnp.where(slope_index < power, leading, between)


def layer_norm(hidden, ln_gain, ln_shift):
    inputs_f32 = hidden.astype(jnp.float32)
    average = jnp.mean(inputs_f32, axis=-1, keepdims=True)
    centred = inputs_f32 - average
    variance = jnp.mean(centred * centred, axis=-1, keepdims=True)
    return (centred * lax.rsqrt(variance + epsilon) * ln_gain + ln_shift).astype(jnp.bfloat16)


def shards(hidden, ln_gain, ln_shift, qkv_weight, qkv_bias, out_weight, out_bias, slope_index):
    seq_rows = hidden.shape[0]
    heads_here = qkv_bias.shape[0]
    head_size = qkv_bias.shape[1] // 3
    flat_width = heads_here * 3 * head_size
    normed = layer_norm(hidden, ln_gain, ln_shift)
    regrouped = lax.all_to_all(qkv_weight, "tp", split_axis=1, concat_axis=0, tiled=True)
    weight_piece = lax.all_gather(regrouped, "rep", axis=0, tiled=True)
    flat_piece = weight_piece.reshape(weight_piece.shape[0], flat_width)
    projected = jnp.dot(normed, flat_piece, preferred_element_type=jnp.float32)
    qkv = (projected.reshape(seq_rows, heads_here, 3 * head_size) + qkv_bias).astype(jnp.bfloat16)
    query = qkv[:, :, :head_size]
    keys = qkv[:, :, head_size : 2 * head_size]
    values = qkv[:, :, 2 * head_size :]
    slopes = slope_values(slope_index)
    scores = jnp.einsum(
        "sha,tha->hst", query, keys, preferred_element_type=jnp.float32
    ) / math.sqrt(head_size)
    position = lax.iota(jnp.int32, seq_rows)
    distance = (position[:, None] - position[None, :]).astype(jnp.float32)
    scores = scores - slopes[:, None, None] * distance
    scores = jnp.where(distance >= 0.0, scores, -1e30)
    highest = jnp.max(scores, axis=-1, keepdims=True)
    powered = jnp.exp(scores - highest)
    attention = (powered / jnp.sum(powered, axis=-1, keepdims=True)).astype(jnp.bfloat16)
    context = jnp.einsum(
        "hst,tha->sha", attention, values, preferred_element_type=jnp.float32
    ).astype(jnp.bfloat16)
    context = context.reshape(seq_rows, heads_here * head_size)
    everything = lax.all_gather(context, "tp", axis=1, tiled=True)
    groups = lax.axis_size("tp")
    group_width = heads_here * head_size
    context_blocks = everything.reshape(seq_rows, groups, group_width)
    weight_blocks = out_weight.reshape(out_weight.shape[0], groups, group_width)
    partials = jnp.einsum(
        "sgk,dgk->gsd", context_blocks, weight_blocks, preferred_element_type=jnp.float32
    ).astype(jnp.bfloat16)
    partials = lax.optimization_barrier(partials)
    result = jnp.sum(partials.astype(jnp.float32), axis=0) + out_bias
    return result.astype(jnp.bfloat16)


def solution(mesh):
    return jax.shard_map(
        shards,
        mesh=mesh,
        in_specs=(
            P("rep", None),
            P(),
            P(),
            P(("rep", "tp"), None, None),
            P("tp", None),
            P("tp", None, None),
            P("tp"),
            P("tp"),
        ),
        out_specs=P("rep", "tp"),
        check_vma=False,
    )
```

profile of v0, /device:TPU:0, one launch (start us, length us, event | category | flops | bytes accessed | tf_op | source)
XLA Modules:
  0.0 449.4 jit_solution(17847641400634748093)
XLA Ops:
  6.5 0.0 all-gather.3.cloned.1.call-start
  6.5 3.9 copy.16
  10.4 128.2 %all_to_all.18 = bf16[448,16,384]{2,0,1:T(8,128)(2,1)S(1)} all-to-all(bf16[448,16,384]{2,0,1:T(8,128)(2,1)S(1)} %copy.16), channel_id=1, replica_groups=mesh['rep'=4,'tp'=8] {'tp'}, dimensions={1} | all-to-all | bytes 11010048 | tf_op jit(solution)/shard_map/all_to_all | solution.py:36
  138.6 3.0 copy.17
  141.6 0.0 all-gather.3.cloned.1.call-update
  141.7 0.0 all-gather.5.cloned.1.call-start
  141.7 0.2 broadcast_compare_fusion
  141.9 0.1 subtract_convert_fusion
  142.1 0.2 copy-done.5
  142.3 7.5 %convert_reduce_fusion = f32[512]{0:T(512)S(1)} fusion(bf16[512,14336]{1,0:T(8,128)(2,1)} %param.8), kind=kLoop, calls=%fused_computation.2 | loop fusion | flops 14679552 | bytes 14682112 | tf_op jit(solution)/shard_map/reduce_sum | solution.py:24
  149.8 12.0 %fusion.3 = f32[512]{0:T(512)S(1)} fusion(bf16[512,14336]{1,0:T(8,128)(2,1)} %param.8, f32[512]{0:T(512)S(1)} %broadcast_multiply_fusion), kind=kLoop, calls=%fused_computation.5 | loop fusion | flops 29359616 | bytes 14684160 | tf_op jit(solution)/shard_map/reduce_sum | solution.py:26
  161.8 0.0 copy-start.2
  161.8 0.0 copy-start.3
  161.8 0.0 copy-start.4
  161.8 180.0 %all-gather.3.cloned.1.call-done = bf16[14336,2,384]{2,0,1:T(8,128)(2,1)} async-done(((bf16[3584,2,384]{2,0,1:T(8,128)(2,1)}), bf16[14336,2,384]{2,0,1:T(8,128)(2,1)}) %all-gather.3.cloned.1.call-update) | async-done | bytes 22020112 | tf_op jit(solution)/shard_map/all_gather | solution.py:37
  341.8 26.1 %copy.18 = bf16[14336,2,384]{0,2,1:T(8,128)(2,1)} copy(bf16[14336,2,384]{2,0,1:T(8,128)(2,1)} %all-gather.3.cloned.1.call-done) | data formatting | bytes 44040192 | tf_op jit(solution)/shard_map/all_gather | solution.py:37
  367.9 0.0 copy-done.2
  367.9 0.0 copy-done.3
  367.9 0.0 copy-done.4
  367.9 17.8 %add_convert_fusion.1 = bf16[512,2,384]{2,0,1:T(8,128)(2,1)S(1)} fusion(bf16[14336,2,384]{0,2,1:T(8,128)(2,1)} %copy.18, bf16[512,14336]{1,0:T(8,128)(2,1)} %param.8, f32[14336]{0:T(1024)S(1)} %copy-done.2, f32[14336]{0:T(1024)S(1)} %copy-done.3, f32[512]{0:T(512)S(1)} %add_rsqrt_fusion, f32[512]{0:T(512)S(1)} %broadcast_multiply_fusion, ...), kind=kOutput, calls=%fused_computation.23 | convolution fusion | flops 11319115776 | bytes 37608448 | tf_op jit(solution)/shard_map/dot_general | solution.py:39
  385.7 0.0 copy-start
  385.7 0.9 copy-done
  386.6 0.6 subtract_select_fusion
  387.2 2.1 fusion.30
  389.2 2.3 convolution_convert_fusion.1
  391.5 0.0 all-gather.5.cloned.1.call-update
  391.6 11.5 %reshape.49 = bf16[1792,8,256]{2,1,0:T(8,128)(2,1)} reshape(bf16[1792,16,128]{2,1,0:T(8,128)(2,1)} %param.13) | data formatting | bytes 14680064 | tf_op jit(solution)/shard_map/reshape | solution.py:63
  403.1 17.8 %all-gather.5.cloned.1.call-done = bf16[512,2048]{0,1:T(8,128)(2,1)} async-done(((bf16[512,256]{0,1:T(8,128)(2,1)}), bf16[512,2048]{0,1:T(8,128)(2,1)}) %all-gather.5.cloned.1.call-update) | async-done | bytes 2097168 | tf_op jit(solution)/shard_map/all_gather | solution.py:59
  420.9 12.1 %convolution_convert_fusion = bf16[8,512,1792]{2,1,0:T(8,128)(2,1)} fusion(bf16[512,8,256]{0,2,1:T(8,128)(2,1)} %bitcast.26, bf16[1792,8,256]{2,1,0:T(8,128)(2,1)} %reshape.49), kind=kOutput, calls=%fused_computation.17 | convolution fusion | flops 3765436416 | bytes 24117248 | tf_op jit(solution)/shard_map/sgk,dgk->gsd/dot_general | solution.py:64
  432.9 8.1 %convert_reduce_fusion.1 = f32[512,1792]{1,0:T(8,128)S(1)} fusion(bf16[8,512,1792]{2,1,0:T(8,128)(2,1)} %convolution_convert_fusion), kind=kLoop, calls=%fused_computation.9 | loop fusion | flops 13762560 | bytes 18350080 | tf_op jit(solution)/shard_map/reduce_sum | solution.py:68
  441.1 0.0 copy-done.1
  441.1 1.5 add_convert_fusion
  (5 shorter events, 0.0 us)
Async XLA Ops:
  6.5 335.3 %all-gather.3.cloned.1.call-start = ((), (), s32[]{:S(2)}) async-start(), calls=%async_computation.1 | async-start | bytes 27525120 | tf_op jit(solution)/shard_map/all_gather | solution.py:37
  141.6 0.7 copy-start.5
  141.7 279.2 %all-gather.5.cloned.1.call-start = ((), (), s32[]{:S(2)}) async-start(), calls=%async_computation.2 | async-start | bytes 2359296 | tf_op jit(solution)/shard_map/all_gather | solution.py:59
  161.8 206.1 %copy-start.2 = (f32[14336]{0:T(1024)S(1)}, f32[14336]{0:T(1024)}, u32[]{:S(2)}) copy-start(f32[14336]{0:T(1024)} %param.10) | copy-start | bytes 172036
  161.8 206.1 %copy-start.3 = (f32[14336]{0:T(1024)S(1)}, f32[14336]{0:T(1024)}, u32[]{:S(2)}) copy-start(f32[14336]{0:T(1024)} %param.9) | copy-start | bytes 172036
  161.8 206.1 %copy-start.4 = (f32[2,384]{1,0:T(2,128)S(1)}, f32[2,384]{1,0:T(2,128)}, u32[]{:S(2)}) copy-start(f32[2,384]{1,0:T(2,128)} %param.12) | copy-start | bytes 9220
  385.7 0.9 copy-start
  432.9 8.1 %copy-start.1 = (f32[1792]{0:T(1024)S(1)}, f32[1792]{0:T(1024)}, u32[]{:S(2)}) copy-start(f32[1792]{0:T(1024)} %param.14) | copy-start | bytes 21508
Sparse Core Ops, SparseCore 0:
  141.8 199.9 all-gather.2
  391.7 29.1 all-gather.4
where the time goes:
time: 451 us; the launch traced here: 449 us
  waiting for transfers between devices  198 us (44%)
  blocking collectives  128 us (28%)
  local copies, waits for them, and re-layouts  45.6 us (10%)
  matrix products  34.8 us (8%)
  other arithmetic  29.5 us (7%)
  between operations  13.5 us (3%)
    all_gather x1, waiting for transfers between devices, shards(): weight_piece = lax.all_gather(regrouped, 'rep', axis=0, tiled=True)  180 us
    all_to_all x1, blocking collectives, shards(): lax.all_to_all(qkv_weight, 'tp', split_axis=1, concat_axis=0, tiled=True)  128 us
    all_gather x1, local copies, waits for them, and re-layouts, shards(): weight_piece = lax.all_gather(regrouped, 'rep', axis=0, tiled=True)  26.1 us
    dot_general x1, matrix products, shards(): projected = jnp.dot(normed, flat_piece, preferred_element_type=jnp.float32)  17.8 us
    all_gather x1, waiting for transfers between devices, shards(): everything = lax.all_gather(context, 'tp', axis=1, tiled=True)  17.8 us
    dot_general x1, matrix products, shards(): jnp.einsum('sgk,dgk->gsd', context_blocks, weight_blocks, preferred_eleme...  12.1 us
    reduce_sum x1, other arithmetic, layer_norm(): variance = jnp.mean(centred * centred, axis=-1, keepdims=True)  12 us
    reshape x1, local copies, waits for them, and re-layouts, shards(): weight_blocks = out_weight.reshape(out_weight.shape[0], groups, group_width)  11.5 us
  transfers between devices with their start and end apart: 2, of which 2 were waited for; matrix products, arithmetic and copies ran while one was open for 7% of the time, Pallas kernels for 0%

commit v1 on v0

v1 whole, which is shorter than its diff:
```python
import functools
import math

import jax
import jax.numpy as jnp
from jax import lax
from jax.experimental import pallas as pl
from jax.experimental.pallas import tpu as pltpu
from jax.sharding import PartitionSpec as P

N_SLOPES = 112
MESH = pl.DeviceIdType.MESH

epsilon = 1e-05


def slope_values(slope_index):
    power = 1 << N_SLOPES.bit_length() - 1
    index_float = slope_index.astype(jnp.float32)
    leading = jnp.exp2(-8.0 * (index_float + 1.0) / power)
    between = jnp.exp2(-4.0 * (2.0 * (index_float - power) + 1.0) / power)
    return jnp.where(slope_index < power, leading, between)


def fused(
    R, T, hidden, gain, shift, weight, bias, slopes, out,
    hid, nsend, xb, wv, psend, precv, acc, ctx,
    lsem, wsend, wrecv, xsend, xrecv, fsend, frecv, psends, precvs, csend, crecv, gsend, grecv,
):
    r = lax.axis_index("rep")
    t = lax.axis_index("tp")
    core = lax.rem(t, 2)
    partner = t + 1 - 2 * core
    heads, depth = weight.shape[1], weight.shape[2]
    half = hid.shape[0]
    seq = 2 * half
    width = xb.shape[2]
    total = R * width
    size = bias.shape[2] // 3
    chips = T // 2
    mine = pl.ds(pl.multiple_of(core * half, half), half)

    load = pltpu.make_async_copy(hidden.at[mine, :], hid, lsem.at[0])
    load.start()

    barrier = pltpu.get_barrier_semaphore()
    for k in range(1, T):
        pl.semaphore_signal(barrier, inc=1, device_id={"tp": lax.rem(t + k, T)}, device_id_type=MESH)
    for j in range(1, R):
        pl.semaphore_signal(barrier, inc=1, device_id={"rep": lax.rem(r + j, R)}, device_id_type=MESH)
    pl.semaphore_wait(barrier, T + R - 2)

    own_rows = pl.ds(pl.multiple_of(t * depth, 16), depth)

    def weight_copy(h, k):
        peer = lax.rem(t + k + 1, T)
        return pltpu.make_async_remote_copy(
            src_ref=weight.at[peer, h],
            dst_ref=wv.at[h, own_rows, :],
            send_sem=wsend.at[h, k],
            recv_sem=wrecv.at[h, k],
            device_id={"tp": peer},
            device_id_type=MESH,
        )

    def own_weight(h):
        return pltpu.make_async_copy(weight.at[t, h], wv.at[h, own_rows, :], lsem.at[2 + h])

    for h in range(heads):
        for k in range(T - 1):
            weight_copy(h, k).start()
        own_weight(h).start()

    load.wait()
    block = 16

    def norm_rows(i, carry):
        rows = pl.ds(pl.multiple_of(i * block, block), block)
        summed = jnp.zeros((block, 1), jnp.float32)
        for q in range(R):
            piece = hid[rows, q * width : (q + 1) * width].astype(jnp.float32)
            summed += jnp.sum(piece, axis=-1, keepdims=True)
        average = summed / total
        squares = jnp.zeros((block, 1), jnp.float32)
        for q in range(R):
            piece = hid[rows, q * width : (q + 1) * width].astype(jnp.float32) - average
            squares += jnp.sum(piece * piece, axis=-1, keepdims=True)
        scale = lax.rsqrt(squares / total + epsilon)
        for q in range(R):
            cols = slice(q * width, (q + 1) * width)
            piece = hid[rows, cols].astype(jnp.float32) - average
            nsend[q, rows, :] = (piece * scale * gain[:, cols] + shift[:, cols]).astype(jnp.bfloat16)
        return carry

    lax.fori_loop(0, half // block, norm_rows, 0)

    def norm_copy(j):
        peer = lax.rem(r + j + 1, R)
        return pltpu.make_async_remote_copy(
            src_ref=nsend.at[peer],
            dst_ref=xb.at[r, mine, :],
            send_sem=xsend.at[j],
            recv_sem=xrecv.at[j],
            device_id={"rep": peer},
            device_id_type=MESH,
        )

    def forward(j):
        owner = lax.rem(r + R - 1 - j, R)
        return pltpu.make_async_remote_copy(
            src_ref=xb.at[owner, mine, :],
            dst_ref=xb.at[owner, mine, :],
            send_sem=fsend.at[j],
            recv_sem=frecv.at[j],
            device_id={"tp": partner},
            device_id_type=MESH,
        )

    for j in range(R - 1):
        norm_copy(j).start()
    own_norm = pltpu.make_async_copy(nsend.at[r], xb.at[r, mine, :], lsem.at[1])
    own_norm.start()
    own_norm.wait()
    forward(R - 1).start()
    for j in range(R - 1):
        norm_copy(j).wait_recv()
        forward(j).start()

    def partial_copy(h, j):
        owner = lax.rem(r + R - 1 - j, R)
        return pltpu.make_async_remote_copy(
            src_ref=psend.at[h, j],
            dst_ref=precv.at[h, j],
            send_sem=psends.at[h, j],
            recv_sem=precvs.at[h, j],
            device_id={"rep": owner},
            device_id_type=MESH,
        )

    for h in range(heads):
        own_weight(h).wait()
        for k in range(T - 1):
            weight_copy(h, k).wait_recv()

        def project(j, carry, h=h):
            owner = lax.rem(r + R - 1 - j, R)
            if h == 0:
                forward(j).wait_recv()
            product = jnp.dot(xb[owner], wv[h], preferred_element_type=jnp.float32)

            @pl.when(j < R - 1)
            def _():
                psend[h, j] = product.astype(jnp.bfloat16)
                partial_copy(h, j).start()

            @pl.when(j == R - 1)
            def _():
                acc[h] = product

            return carry

        lax.fori_loop(0, R, project, 0)

    def context_cols(source, h):
        return pl.ds(pl.multiple_of(source * (heads * size) + h * size, size), size)

    def context_copy(h, k):
        peer = lax.rem(t + 2 * k + 2, T)
        cols = context_cols(t, h)
        return pltpu.make_async_remote_copy(
            src_ref=ctx.at[:, cols],
            dst_ref=ctx.at[:, cols],
            send_sem=csend.at[h, k],
            recv_sem=crecv.at[h, k],
            device_id={"tp": peer},
            device_id_type=MESH,
        )

    def context_forward(h, k):
        source = lax.rem(t + T - 2 * k, T)
        cols = context_cols(source, h)
        return pltpu.make_async_remote_copy(
            src_ref=ctx.at[:, cols],
            dst_ref=ctx.at[:, cols],
            send_sem=gsend.at[h, k],
            recv_sem=grecv.at[h, k],
            device_id={"tp": partner},
            device_id_type=MESH,
        )

    for h in range(heads):
        for j in range(R - 1):
            partial_copy(h, j).wait_recv()
        joined = acc[h]
        for j in range(R - 1):
            joined += precv[h, j].astype(jnp.float32)
        qkv = (joined + bias[h]).astype(jnp.bfloat16)
        keys = qkv[:, size : 2 * size]
        values = qkv[:, 2 * size :]
        step = min(seq, 128)
        for b in range(seq // step):
            query = qkv[b * step : (b + 1) * step, :size]
            scores = lax.dot_general(
                query, keys, (((1,), (1,)), ((), ())), preferred_element_type=jnp.float32
            ) * (1.0 / math.sqrt(size))
            distance = (
                lax.broadcasted_iota(jnp.int32, (step, seq), 0)
                + b * step
                - lax.broadcasted_iota(jnp.int32, (step, seq), 1)
            )
            scores = scores - slopes[h] * distance.astype(jnp.float32)
            scores = jnp.where(distance >= 0, scores, -1e30)
            highest = jnp.max(scores, axis=-1, keepdims=True)
            powered = jnp.exp(scores - highest)
            attention = (powered / jnp.sum(powered, axis=-1, keepdims=True)).astype(jnp.bfloat16)
            context = jnp.dot(attention, values, preferred_element_type=jnp.float32)
            ctx[b * step : (b + 1) * step, context_cols(t, h)] = context.astype(jnp.bfloat16)
        for k in range(chips - 1):
            context_copy(h, k).start()
        context_forward(h, 0).start()

    for h in range(heads):
        for k in range(1, chips):
            context_copy(h, k - 1).wait_recv()
            context_forward(h, k).start()
    for h in range(heads):
        for k in range(chips):
            context_forward(h, k).wait_recv()
    out[...] = ctx[...]

    for j in range(R):
        forward(j).wait_send()
    for j in range(R - 1):
        norm_copy(j).wait_send()
    for h in range(heads):
        for k in range(T - 1):
            weight_copy(h, k).wait_send()
        for j in range(R - 1):
            partial_copy(h, j).wait_send()
        for k in range(chips - 1):
            context_copy(h, k).wait_send()
        for k in range(chips):
            context_forward(h, k).wait_send()


def shards(hidden, ln_gain, ln_shift, qkv_weight, qkv_bias, out_weight, out_bias, slope_index):
    R, T = lax.axis_size("rep"), lax.axis_size("tp")
    seq, total = hidden.shape
    heads, wide = qkv_bias.shape
    size = wide // 3
    depth = qkv_weight.shape[0]
    width = total // R
    half = seq // 2
    chips = T // 2
    grouped = qkv_weight.reshape(depth, T, heads, wide).transpose(1, 2, 0, 3)
    vmem = pl.BlockSpec(memory_space=pltpu.VMEM)
    hbm = pl.BlockSpec(memory_space=pl.ANY)
    dma = pltpu.SemaphoreType.DMA
    context = pl.pallas_call(
        functools.partial(fused, R, T),
        out_shape=jax.ShapeDtypeStruct((seq, T * heads * size), jnp.bfloat16),
        in_specs=[hbm, vmem, vmem, hbm, vmem, pl.BlockSpec(memory_space=pltpu.SMEM)],
        out_specs=vmem,
        scratch_shapes=[
            pltpu.VMEM((half, total), jnp.bfloat16),
            pltpu.VMEM((R, half, width), jnp.bfloat16),
            pltpu.VMEM((R, seq, width), jnp.bfloat16),
            pltpu.VMEM((heads, width, wide), jnp.bfloat16),
            pltpu.VMEM((heads, R - 1, seq, wide), jnp.bfloat16),
            pltpu.VMEM((heads, R - 1, seq, wide), jnp.bfloat16),
            pltpu.VMEM((heads, seq, wide), jnp.float32),
            pltpu.VMEM((seq, T * heads * size), jnp.bfloat16),
            dma((2 + heads,)),
            dma((heads, T - 1)),
            dma((heads, T - 1)),
            dma((R - 1,)),
            dma((R - 1,)),
            dma((R,)),
            dma((R,)),
            dma((heads, R - 1)),
            dma((heads, R - 1)),
            dma((heads, chips - 1)),
            dma((heads, chips - 1)),
            dma((heads, chips)),
            dma((heads, chips)),
        ],
        compiler_params=pltpu.CompilerParams(
            collective_id=0, has_side_effects=True, vmem_limit_bytes=62 * 1024 * 1024
        ),
    )(
        hidden,
        ln_gain.reshape(1, total),
        ln_shift.reshape(1, total),
        grouped,
        qkv_bias.reshape(heads, 1, wide),
        slope_values(slope_index),
    )
    flat = out_weight.reshape(out_weight.shape[0], -1)
    result = lax.dot_general(
        context, flat, (((1,), (1,)), ((), ())), preferred_element_type=jnp.float32
    )
    return (result + out_bias).astype(jnp.bfloat16)


def solution(mesh):
    return jax.shard_map(
        shards,
        mesh=mesh,
        in_specs=(
            P("rep", None),
            P(),
            P(),
            P(("rep", "tp"), None, None),
            P("tp", None),
            P("tp", None, None),
            P("tp"),
            P("tp"),
        ),
        out_specs=P("rep", "tp"),
        check_vma=False,
    )
```

time: 451 us -> 173 us (0.38)
  waiting for transfers between devices: 198 us -> 0 us
  Pallas kernels: 0 us -> 155 us
  blocking collectives: 128 us -> 0 us
  local copies, waits for them, and re-layouts: 45.6 us -> 7.54 us
  other arithmetic: 29.5 us -> 1.31 us
  matrix products: 34.8 us -> 8.97 us
  between operations: 13.5 us -> 0.02 us
    all_gather x2 -> x0, waiting for transfers between devices: 198 us -> none  [the longest x1 180 us: shards(): weight_piece = lax.all_gather(regrouped, 'rep', axis=0, tiled=True)]
    pallas_call x0 -> x1, Pallas kernels: none -> 155 us  [shards(): pl.pallas_call(functools.partial(fused, R, T), out_shape=jax.ShapeDtypeSt...]
    all_to_all x1 -> x0, blocking collectives: 128 us -> none  [shards(): lax.all_to_all(qkv_weight, 'tp', split_axis=1, concat_axis=0, tiled=True)]
    reduce_sum x3 -> x0, other arithmetic: 27.6 us -> none  [the longest x1 12 us: layer_norm(): variance = jnp.mean(centred * centred, axis=-1, keepdims=True)]
    all_gather x1 -> x0, local copies, waits for them, and re-layouts: 26.1 us -> none  [shards(): weight_piece = lax.all_gather(regrouped, 'rep', axis=0, tiled=True)]
    dot_general x4 -> x1, matrix products: 32.8 us -> 8.97 us  [shards(): lax.dot_general(context, flat, (((1,), (1,)), ((), ())), preferred_elemen...]
    reshape x1, local copies, waits for them, and re-layouts: 11.5 us -> 1.26 us  [shards(): qkv_bias.reshape(heads, 1, wide)]
  transfers between devices with their start and end apart: 2 -> 0, of which waited for: 2 -> 0; matrix products, arithmetic and copies ran while one was open for 7% -> 0% of each run, Pallas kernels for 0% -> 0%
where the time goes in v1:
time: 173 us
  Pallas kernels  155 us (90%)
  matrix products  8.97 us (5%)
  local copies, waits for them, and re-layouts  7.54 us (4%)
    pallas_call x1, Pallas kernels, shards(): pl.pallas_call(functools.partial(fused, R, T), out_shape=jax.ShapeDtypeSt...  155 us
    dot_general x1, matrix products, shards(): lax.dot_general(context, flat, (((1,), (1,)), ((), ())), preferred_elemen...  8.97 us
    unnamed x3, local copies, waits for them, and re-layouts  6.27 us

profile of v1, /device:TPU:0, one launch (start us, length us, event | category | flops | bytes accessed | tf_op | source)
XLA Modules:
  0.0 172.6 jit_solution(216078293766707763)
XLA Ops:
  0.0 1.3 compare_select_fusion.slopes
  1.3 1.3 reshape.19.bias
  2.6 6.3 %copy.9 = bf16[448,16,384]{2,0,1:T(8,128)(2,1)} copy(bf16[448,16,384]{2,1,0:T(8,128)(2,1)} %param.11) | data formatting | bytes 11010048 | tf_op args[3]
  8.8 0.0 copy-start
  8.8 154.8 %shard_map.82 = bf16[512,2048]{1,0:T(8,128)(2,1)} custom-call(bf16[512,14336]{1,0:T(8,128)(2,1)} %hidden.1, f32[1,14336]{1,0:T(1,128)} %bitcast.13, f32[1,14336]{1,0:T(1,128)} %bitcast.14, bf16[8,2,448,384]{3,2,1,0:T(8,128)(2,1)} %bitcast.12, f32[2,1,384]{2,1,0:T(1,128)} %reshape.19.bias, f32[2]{0:T(128)} %compare_select_fusion.slopes), custom_call_target="tpu_custom_call" | custom-call | tf_op jit(solution)/shard_map/pallas_call | solution.py:259
  163.6 0.0 copy-done
  163.7 9.0 %add_convert_fusion = bf16[512,1792]{1,0:T(8,128)(2,1)} fusion(bf16[512,2048]{1,0:T(8,128)(2,1)} %shard_map.82, bf16[224,8,16,128]{3,2,1,0:T(8,128)(2,1)} %bitcast.15, f32[1792]{0:T(1024)S(1)} %copy-done), kind=kOutput, calls=%fused_computation.3 | convolution fusion | flops 3759931392 | bytes 11279360 | tf_op jit(solution)/shard_map/dot_general | solution.py:299
Async XLA Ops:
  8.8 154.8 %copy-start = (f32[1792]{0:T(1024)S(1)}, f32[1792]{0:T(1024)}, u32[]{:S(2)}) copy-start(f32[1792]{0:T(1024)} %param.14) | copy-start | bytes 21508

commit v2 on v1

v2 whole, which is shorter than its diff:
```python
import functools
import math

import jax
import jax.numpy as jnp
from jax import lax
from jax.experimental import pallas as pl
from jax.experimental.pallas import tpu as pltpu
from jax.sharding import PartitionSpec as P

N_SLOPES = 112
MESH = pl.DeviceIdType.MESH

epsilon = 1e-05


def slope_values(slope_index):
    power = 1 << N_SLOPES.bit_length() - 1
    index_float = slope_index.astype(jnp.float32)
    leading = jnp.exp2(-8.0 * (index_float + 1.0) / power)
    between = jnp.exp2(-4.0 * (2.0 * (index_float - power) + 1.0) / power)
    return jnp.where(slope_index < power, leading, between)


def fused(
    R, T, C, pieces, hidden, gain, shift, weight, bias, slope_index, out,
    hid, nsend, xb, psend, precv, acc, att, ctx, wv,
    lsem, osem, wsend, wrecv, xsend, xrecv, fsend, frecv, psends, precvs, csend, crecv, gsend, grecv,
):
    r = lax.axis_index("rep")
    t = lax.axis_index("tp")
    core = lax.rem(t, 2)
    partner = t + 1 - 2 * core
    heads, depth = weight.shape[1], weight.shape[2]
    half = hid.shape[0]
    seq = 2 * half
    width = xb.shape[2]
    total = R * width
    size = bias.shape[1] // 3
    chips = T // 2
    part = half // C
    mine = pl.ds(pl.multiple_of(core * half, half), half)

    def part_rows(c):
        return pl.ds(c * part, part)

    def part_mine(c):
        return pl.ds(pl.multiple_of(core * half + c * part, part), part)

    def load(c):
        return pltpu.make_async_copy(hidden.at[part_mine(c), :], hid.at[part_rows(c), :], lsem.at[c])

    for c in range(C):
        load(c).start()

    barrier = pltpu.get_barrier_semaphore()
    for k in range(1, T):
        pl.semaphore_signal(barrier, inc=1, device_id={"tp": lax.rem(t + k, T)}, device_id_type=MESH)
    for j in range(1, R):
        pl.semaphore_signal(barrier, inc=1, device_id={"rep": lax.rem(r + j, R)}, device_id_type=MESH)
    pl.semaphore_wait(barrier, T + R - 2)

    own_rows = pl.ds(pl.multiple_of(t * depth, 16), depth)

    def weight_copy(p, k):
        h, first, count = pieces[p]
        peer = lax.rem(t + k + 1, T)
        return pltpu.make_async_remote_copy(
            src_ref=weight.at[peer, h, :, pl.ds(first, count)],
            dst_ref=wv.at[h, own_rows, pl.ds(first, count)],
            send_sem=wsend.at[p, k],
            recv_sem=wrecv.at[p, k],
            device_id={"tp": peer},
            device_id_type=MESH,
        )

    def own_weight(h):
        return pltpu.make_async_copy(weight.at[t, h], wv.at[h, own_rows, :], osem.at[h])

    for p in range(len(pieces)):
        for k in range(T - 1):
            weight_copy(p, k).start()
    for h in range(heads):
        own_weight(h).start()

    def norm_copy(j, c):
        peer = lax.rem(r + j + 1, R)
        return pltpu.make_async_remote_copy(
            src_ref=nsend.at[peer, part_rows(c), :],
            dst_ref=xb.at[r, part_mine(c), :],
            send_sem=xsend.at[j, c],
            recv_sem=xrecv.at[j, c],
            device_id={"rep": peer},
            device_id_type=MESH,
        )

    def forward(j, c):
        owner = lax.rem(r + R - 1 - j, R)
        source = xb.at[owner, part_mine(c), :]
        if j == R - 1:
            source = nsend.at[r, part_rows(c), :]
        return pltpu.make_async_remote_copy(
            src_ref=source,
            dst_ref=xb.at[owner, part_mine(c), :],
            send_sem=fsend.at[j, c],
            recv_sem=frecv.at[j, c],
            device_id={"tp": partner},
            device_id_type=MESH,
        )

    def own_norm(c):
        return pltpu.make_async_copy(
            nsend.at[r, part_rows(c), :], xb.at[r, part_mine(c), :], lsem.at[C + c]
        )

    block = 16

    def norm_rows(i, carry):
        rows = pl.ds(pl.multiple_of(i * block, block), block)
        summed = jnp.zeros((block, 1), jnp.float32)
        for q in range(R):
            piece = hid[rows, q * width : (q + 1) * width].astype(jnp.float32)
            summed += jnp.sum(piece, axis=-1, keepdims=True)
        average = summed / total
        squares = jnp.zeros((block, 1), jnp.float32)
        for q in range(R):
            piece = hid[rows, q * width : (q + 1) * width].astype(jnp.float32) - average
            squares += jnp.sum(piece * piece, axis=-1, keepdims=True)
        scale = lax.rsqrt(squares / total + epsilon)
        for q in range(R):
            cols = slice(q * width, (q + 1) * width)
            piece = hid[rows, cols].astype(jnp.float32) - average
            nsend[q, rows, :] = (piece * scale * gain[:, cols] + shift[:, cols]).astype(jnp.bfloat16)
        return carry

    for c in range(C):
        load(c).wait()
        lax.fori_loop(c * part // block, (c + 1) * part // block, norm_rows, 0)
        for j in range(R - 1):
            norm_copy(j, c).start()
        own_norm(c).start()
        forward(R - 1, c).start()
    for c in range(C):
        for j in range(R - 1):
            norm_copy(j, c).wait_recv()
            forward(j, c).start()
    for c in range(C):
        own_norm(c).wait()
        for j in range(R):
            forward(j, c).wait_recv()

    def partial_copy(p, j):
        h, first, count = pieces[p]
        owner = lax.rem(r + R - 1 - j, R)
        return pltpu.make_async_remote_copy(
            src_ref=psend.at[h, j, :, pl.ds(first, count)],
            dst_ref=precv.at[h, j, :, pl.ds(first, count)],
            send_sem=psends.at[p, j],
            recv_sem=precvs.at[p, j],
            device_id={"rep": owner},
            device_id_type=MESH,
        )

    def project_piece(p):
        h, first, count = pieces[p]
        cols = slice(first, first + count)

        def project(j, carry):
            owner = lax.rem(r + R - 1 - j, R)
            product = jnp.dot(xb[owner], wv[h, :, cols], preferred_element_type=jnp.float32)

            @pl.when(j < R - 1)
            def _():
                psend[h, j, :, cols] = product.astype(jnp.bfloat16)
                partial_copy(p, j).start()

            @pl.when(j == R - 1)
            def _():
                acc[h, :, cols] = product

            return carry

        lax.fori_loop(0, R, project, 0)

    def wait_weight(p):
        if pieces[p][1] == 0:
            own_weight(pieces[p][0]).wait()
        for k in range(T - 1):
            weight_copy(p, k).wait_recv()

    def joined(h, first, count):
        cols = slice(first, first + count)
        result = acc[h, :, cols]
        for j in range(R - 1):
            result += precv[h, j, :, cols].astype(jnp.float32)
        return (result + bias[h : h + 1, cols]).astype(jnp.bfloat16)

    def context_cols(source, h):
        return pl.ds(pl.multiple_of(source * (heads * size) + h * size, size), size)

    def context_copy(h, k):
        peer = lax.rem(t + 2 * k + 2, T)
        cols = context_cols(t, h)
        return pltpu.make_async_remote_copy(
            src_ref=ctx.at[:, cols],
            dst_ref=ctx.at[:, cols],
            send_sem=csend.at[h, k],
            recv_sem=crecv.at[h, k],
            device_id={"tp": peer},
            device_id_type=MESH,
        )

    def context_forward(h, k):
        source = lax.rem(t + T - 2 * k, T)
        cols = context_cols(source, h)
        return pltpu.make_async_remote_copy(
            src_ref=ctx.at[:, cols],
            dst_ref=ctx.at[:, cols],
            send_sem=gsend.at[h, k],
            recv_sem=grecv.at[h, k],
            device_id={"tp": partner},
            device_id_type=MESH,
        )

    def attend(h):
        both = joined(h, 0, 2 * size)
        keys = both[:, size:]
        index = jnp.full((1, seq), slope_index[h], jnp.int32)
        slope = slope_values(index)
        step = min(seq, 128)
        for b in range(seq // step):
            query = both[b * step : (b + 1) * step, :size]
            scores = lax.dot_general(
                query, keys, (((1,), (1,)), ((), ())), preferred_element_type=jnp.float32
            ) * (1.0 / math.sqrt(size))
            distance = (
                lax.broadcasted_iota(jnp.int32, (step, seq), 0)
                + b * step
                - lax.broadcasted_iota(jnp.int32, (step, seq), 1)
            )
            scores = scores - slope * distance.astype(jnp.float32)
            scores = jnp.where(distance >= 0, scores, -1e30)
            highest = jnp.max(scores, axis=-1, keepdims=True)
            powered = jnp.exp(scores - highest)
            att[b * step : (b + 1) * step, :] = (
                powered / jnp.sum(powered, axis=-1, keepdims=True)
            ).astype(jnp.bfloat16)

    def combine(h):
        values = joined(h, 2 * size, size)
        context = jnp.dot(att[...], values, preferred_element_type=jnp.float32)
        ctx[:, context_cols(t, h)] = context.astype(jnp.bfloat16)

    def send_context(h):
        for k in range(chips - 1):
            context_copy(h, k).start()
        context_forward(h, 0).start()

    last = len(pieces) - 1
    for p in range(last):
        wait_weight(p)
        project_piece(p)
    for p in range(last):
        for j in range(R - 1):
            partial_copy(p, j).wait_recv()
        h = pieces[p][0]
        attend(h)
        if p < last - 1:
            combine(h)
    wait_weight(last)
    for h in range(heads - 1):
        send_context(h)
    project_piece(last)
    for j in range(R - 1):
        partial_copy(last, j).wait_recv()
    combine(heads - 1)
    send_context(heads - 1)

    for h in range(heads):
        for k in range(1, chips):
            context_copy(h, k - 1).wait_recv()
            context_forward(h, k).start()
    for h in range(heads):
        for k in range(chips):
            context_forward(h, k).wait_recv()
    out[...] = ctx[...]

    for c in range(C):
        for j in range(R):
            forward(j, c).wait_send()
        for j in range(R - 1):
            norm_copy(j, c).wait_send()
    for p in range(len(pieces)):
        for k in range(T - 1):
            weight_copy(p, k).wait_send()
        for j in range(R - 1):
            partial_copy(p, j).wait_send()
    for h in range(heads):
        for k in range(chips - 1):
            context_copy(h, k).wait_send()
        for k in range(chips):
            context_forward(h, k).wait_send()


def shards(hidden, ln_gain, ln_shift, qkv_weight, qkv_bias, out_weight, out_bias, slope_index):
    R, T = lax.axis_size("rep"), lax.axis_size("tp")
    seq, total = hidden.shape
    heads, wide = qkv_bias.shape
    size = wide // 3
    depth = qkv_weight.shape[0]
    width = total // R
    half = seq // 2
    chips = T // 2
    C = 4
    pieces = [(h, 0, wide) for h in range(heads - 1)]
    pieces += [(heads - 1, 0, 2 * size), (heads - 1, 2 * size, size)]
    count = len(pieces)
    grouped = qkv_weight.reshape(depth, T, heads, wide).transpose(1, 2, 0, 3)
    vmem = pl.BlockSpec(memory_space=pltpu.VMEM)
    hbm = pl.BlockSpec(memory_space=pl.ANY)
    dma = pltpu.SemaphoreType.DMA
    context = pl.pallas_call(
        functools.partial(fused, R, T, C, pieces),
        out_shape=jax.ShapeDtypeStruct((seq, T * heads * size), jnp.bfloat16),
        in_specs=[hbm, vmem, vmem, hbm, vmem, pl.BlockSpec(memory_space=pltpu.SMEM)],
        out_specs=vmem,
        scratch_shapes=[
            pltpu.VMEM((half, total), jnp.bfloat16),
            pltpu.VMEM((R, half, width), jnp.bfloat16),
            pltpu.VMEM((R, seq, width), jnp.bfloat16),
            pltpu.VMEM((heads, R - 1, seq, wide), jnp.bfloat16),
            pltpu.VMEM((heads, R - 1, seq, wide), jnp.bfloat16),
            pltpu.VMEM((heads, seq, wide), jnp.float32),
            pltpu.VMEM((seq, seq), jnp.bfloat16),
            pltpu.VMEM((seq, T * heads * size), jnp.bfloat16),
            pltpu.VMEM((heads, width, wide), jnp.bfloat16),
            dma((2 * C,)),
            dma((heads,)),
            dma((count, T - 1)),
            dma((count, T - 1)),
            dma((R - 1, C)),
            dma((R - 1, C)),
            dma((R, C)),
            dma((R, C)),
            dma((count, R - 1)),
            dma((count, R - 1)),
            dma((heads, chips - 1)),
            dma((heads, chips - 1)),
            dma((heads, chips)),
            dma((heads, chips)),
        ],
        compiler_params=pltpu.CompilerParams(
            collective_id=0, has_side_effects=True, vmem_limit_bytes=62 * 1024 * 1024
        ),
    )(
        hidden,
        ln_gain.reshape(1, total),
        ln_shift.reshape(1, total),
        grouped,
        qkv_bias,
        slope_index,
    )
    flat = out_weight.reshape(out_weight.shape[0], -1)
    result = lax.dot_general(
        context, flat, (((1,), (1,)), ((), ())), preferred_element_type=jnp.float32
    )
    return (result + out_bias).astype(jnp.bfloat16)


def solution(mesh):
    return jax.shard_map(
        shards,
        mesh=mesh,
        in_specs=(
            P("rep", None),
            P(),
            P(),
            P(("rep", "tp"), None, None),
            P("tp", None),
            P("tp", None, None),
            P("tp"),
            P("tp"),
        ),
        out_specs=P("rep", "tp"),
        check_vma=False,
    )
```

time: 173 us -> 167 us (0.965)
  Pallas kernels: 155 us -> 152 us
    pallas_call x1, Pallas kernels: 155 us -> 152 us  [shards(): pl.pallas_call(functools.partial(fused, R, T, C, pieces), out_shape=jax.S...]
where the time goes in v2:
time: 167 us
  Pallas kernels  152 us (91%)
  matrix products  8.96 us (5%)
  local copies, waits for them, and re-layouts  6.27 us (4%)
    pallas_call x1, Pallas kernels, shards(): pl.pallas_call(functools.partial(fused, R, T, C, pieces), out_shape=jax.S...  152 us
    dot_general x1, matrix products, shards(): lax.dot_general(context, flat, (((1,), (1,)), ((), ())), preferred_elemen...  8.96 us
    unnamed x3, local copies, waits for them, and re-layouts  6.27 us

profile of v2, /device:TPU:0, one launch (start us, length us, event | category | flops | bytes accessed | tf_op | source)
XLA Modules:
  0.0 166.9 jit_solution(66457419957830651)
XLA Ops:
  0.0 6.3 %copy.9 = bf16[448,16,384]{2,0,1:T(8,128)(2,1)} copy(bf16[448,16,384]{2,1,0:T(8,128)(2,1)} %param.11) | data formatting | bytes 11010048 | tf_op args[3]
  6.3 0.0 copy-start
  6.3 151.7 %shard_map.82 = bf16[512,2048]{1,0:T(8,128)(2,1)} custom-call(bf16[512,14336]{1,0:T(8,128)(2,1)} %hidden.1, f32[1,14336]{1,0:T(1,128)} %bitcast.13, f32[1,14336]{1,0:T(1,128)} %bitcast.14, bf16[8,2,448,384]{3,2,1,0:T(8,128)(2,1)} %bitcast.12, f32[2,384]{1,0:T(2,128)} %bias.1, s32[2]{0:T(128)} %slope_index.1), custom_call_target="tpu_custom_call" | custom-call | tf_op jit(solution)/shard_map/pallas_call | solution.py:322
  157.9 0.0 copy-done
  158.0 9.0 %add_convert_fusion = bf16[512,1792]{1,0:T(8,128)(2,1)} fusion(bf16[512,2048]{1,0:T(8,128)(2,1)} %shard_map.82, bf16[224,8,16,128]{3,2,1,0:T(8,128)(2,1)} %bitcast.15, f32[1792]{0:T(1024)S(1)} %copy-done), kind=kOutput, calls=%fused_computation.3 | convolution fusion | flops 3759931392 | bytes 11279360 | tf_op jit(solution)/shard_map/dot_general | solution.py:364
Async XLA Ops:
  6.3 151.7 %copy-start = (f32[1792]{0:T(1024)S(1)}, f32[1792]{0:T(1024)}, u32[]{:S(2)}) copy-start(f32[1792]{0:T(1024)} %param.14) | copy-start | bytes 21508

commit v3 on v2

--- a/solution.py
+++ b/solution.py
@@ -23,15 +23,15 @@
 
 
 def fused(
-    R, T, C, pieces, hidden, gain, shift, weight, bias, slope_index, out,
-    hid, nsend, xb, psend, precv, acc, att, ctx, wv,
-    lsem, osem, wsend, wrecv, xsend, xrecv, fsend, frecv, psends, precvs, csend, crecv, gsend, grecv,
+    R, T, C, pieces, parts, units, hidden, gain, shift, weight, bias, slope_index, proj, out, flat,
+    hid, nsend, xb, psend, precv, acc, att, ctx, wv, vals, stage, staged,
+    isem, jsem, lsem, osem, wsend, wrecv, xsend, xrecv, fsend, frecv, psends, precvs, csend, crecv, gsend, grecv,
 ):
     r = lax.axis_index("rep")
     t = lax.axis_index("tp")
     core = lax.rem(t, 2)
     partner = t + 1 - 2 * core
-    heads, depth = weight.shape[1], weight.shape[2]
+    heads, depth = wv.shape[0], weight.shape[2]
     half = hid.shape[0]
     seq = 2 * half
     width = xb.shape[2]
@@ -53,6 +53,19 @@
     for c in range(C):
         load(c).start()
 
+    chunk = stage.shape[1]
+
+    def stage_in(i):
+        rows = pl.ds(i * chunk, chunk)
+        return pltpu.make_async_copy(proj.at[rows], stage.at[i % 2], isem.at[i % 2])
+
+    def stage_out(i):
+        rows = pl.ds(i * chunk, chunk)
+        return pltpu.make_async_copy(staged.at[i % 2], flat.at[rows, :], jsem.at[i % 2])
+
+    for i in range(2):
+        stage_in(i).start()
+
     barrier = pltpu.get_barrier_semaphore()
     for k in range(1, T):
         pl.semaphore_signal(barrier, inc=1, device_id={"tp": lax.rem(t + k, T)}, device_id_type=MESH)
@@ -77,10 +90,11 @@
     def own_weight(h):
         return pltpu.make_async_copy(weight.at[t, h], wv.at[h, own_rows, :], osem.at[h])
 
-    for p in range(len(pieces)):
-        for k in range(T - 1):
-            weight_copy(p, k).start()
     for h in range(heads):
+        for p in range(len(pieces)):
+            if pieces[p][0] == h:
+                for k in range(T - 1):
+                    weight_copy(p, k).start()
         own_weight(h).start()
 
     def norm_copy(j, c):
@@ -140,6 +154,26 @@
             norm_copy(j, c).start()
         own_norm(c).start()
         forward(R - 1, c).start()
+
+    steps = proj.shape[0] // chunk
+    for i in range(steps):
+        stage_in(i).wait()
+        if i >= 2:
+            stage_out(i - 2).wait()
+
+        def flatten(b, carry, slot=i % 2):
+            rows = pl.ds(pl.multiple_of(b * 16, 16), 16)
+            for g in range(proj.shape[1]):
+                staged[slot, rows, g * size : (g + 1) * size] = stage[slot, rows, g, :]
+            return carry
+
+        lax.fori_loop(0, chunk // 16, flatten, 0)
+        stage_out(i).start()
+        if i + 2 < steps:
+            stage_in(i + 2).start()
+    for i in range(max(steps - 2, 0), steps):
+        stage_out(i).wait()
+
     for c in range(C):
         for j in range(R - 1):
             norm_copy(j, c).wait_recv()
@@ -149,34 +183,36 @@
         for j in range(R):
             forward(j, c).wait_recv()
 
-    def partial_copy(p, j):
-        h, first, count = pieces[p]
+    def partial_copy(q, j):
+        h, first, count, top, tall = parts[q]
         owner = lax.rem(r + R - 1 - j, R)
-        return pltpu.make_async_remote_copy(
-            src_ref=psend.at[h, j, :, pl.ds(first, count)],
-            dst_ref=precv.at[h, j, :, pl.ds(first, count)],
-            send_sem=psends.at[p, j],
-            recv_sem=precvs.at[p, j],
+        area = (h, j, pl.ds(top, tall), pl.ds(first, count))
+        return pltpu.make_async_remote_copy(
+            src_ref=psend.at[area],
+            dst_ref=precv.at[area],
+            send_sem=psends.at[q, j],
+            recv_sem=precvs.at[q, j],
             device_id={"rep": owner},
             device_id_type=MESH,
         )
 
-    def project_piece(p):
-        h, first, count = pieces[p]
+    def project_part(q):
+        h, first, count, top, tall = parts[q]
         cols = slice(first, first + count)
+        rows = slice(top, top + tall)
 
         def project(j, carry):
             owner = lax.rem(r + R - 1 - j, R)
-            product = jnp.dot(xb[owner], wv[h, :, cols], preferred_element_type=jnp.float32)
+            product = jnp.dot(xb[owner, rows], wv[h, :, cols], preferred_element_type=jnp.float32)
 
             @pl.when(j < R - 1)
             def _():
-                psend[h, j, :, cols] = product.astype(jnp.bfloat16)
-                partial_copy(p, j).start()
+                psend[h, j, rows, cols] = product.astype(jnp.bfloat16)
+                partial_copy(q, j).start()
 
             @pl.when(j == R - 1)
             def _():
-                acc[h, :, cols] = product
+                acc[h, rows, cols] = product
 
             return carry
 
@@ -188,42 +224,45 @@
         for k in range(T - 1):
             weight_copy(p, k).wait_recv()
 
-    def joined(h, first, count):
+    def joined(h, first, count, top, tall):
         cols = slice(first, first + count)
-        result = acc[h, :, cols]
-        for j in range(R - 1):
-            result += precv[h, j, :, cols].astype(jnp.float32)
+        rows = slice(top, top + tall)
+        result = acc[h, rows, cols]
+        for j in range(R - 1):
+            result += precv[h, j, rows, cols].astype(jnp.float32)
         return (result + bias[h : h + 1, cols]).astype(jnp.bfloat16)
 
     def context_cols(source, h):
         return pl.ds(pl.multiple_of(source * (heads * size) + h * size, size), size)
 
-    def context_copy(h, k):
+    def context_copy(u, k):
+        h, top, tall = units[u]
         peer = lax.rem(t + 2 * k + 2, T)
-        cols = context_cols(t, h)
-        return pltpu.make_async_remote_copy(
-            src_ref=ctx.at[:, cols],
-            dst_ref=ctx.at[:, cols],
-            send_sem=csend.at[h, k],
-            recv_sem=crecv.at[h, k],
+        area = (pl.ds(top, tall), context_cols(t, h))
+        return pltpu.make_async_remote_copy(
+            src_ref=ctx.at[area],
+            dst_ref=ctx.at[area],
+            send_sem=csend.at[u, k],
+            recv_sem=crecv.at[u, k],
             device_id={"tp": peer},
             device_id_type=MESH,
         )
 
-    def context_forward(h, k):
+    def context_forward(u, k):
+        h, top, tall = units[u]
         source = lax.rem(t + T - 2 * k, T)
-        cols = context_cols(source, h)
-        return pltpu.make_async_remote_copy(
-            src_ref=ctx.at[:, cols],
-            dst_ref=ctx.at[:, cols],
-            send_sem=gsend.at[h, k],
-            recv_sem=grecv.at[h, k],
+        area = (pl.ds(top, tall), context_cols(source, h))
+        return pltpu.make_async_remote_copy(
+            src_ref=ctx.at[area],
+            dst_ref=ctx.at[area],
+            send_sem=gsend.at[u, k],
+            recv_sem=grecv.at[u, k],
             device_id={"tp": partner},
             device_id_type=MESH,
         )
 
     def attend(h):
-        both = joined(h, 0, 2 * size)
+        both = joined(h, 0, 2 * size, 0, seq)
         keys = both[:, size:]
         index = jnp.full((1, seq), slope_index[h], jnp.int32)
         slope = slope_values(index)
@@ -246,44 +285,49 @@
                 powered / jnp.sum(powered, axis=-1, keepdims=True)
             ).astype(jnp.bfloat16)
 
-    def combine(h):
-        values = joined(h, 2 * size, size)
-        context = jnp.dot(att[...], values, preferred_element_type=jnp.float32)
-        ctx[:, context_cols(t, h)] = context.astype(jnp.bfloat16)
-
-    def send_context(h):
+    def combine(u):
+        h, top, tall = units[u]
+        rows = slice(top, top + tall)
+        vals[rows, :] = joined(h, 2 * size, size, top, tall)
+        reach = top + tall
+        context = jnp.dot(att[rows, :reach], vals[:reach, :], preferred_element_type=jnp.float32)
+        ctx[rows, context_cols(t, h)] = context.astype(jnp.bfloat16)
+
+    def send_context(u):
         for k in range(chips - 1):
-            context_copy(h, k).start()
-        context_forward(h, 0).start()
+            context_copy(u, k).start()
+        context_forward(u, 0).start()
 
     last = len(pieces) - 1
     for p in range(last):
         wait_weight(p)
-        project_piece(p)
+        project_part(p)
     for p in range(last):
         for j in range(R - 1):
             partial_copy(p, j).wait_recv()
-        h = pieces[p][0]
-        attend(h)
+        attend(pieces[p][0])
         if p < last - 1:
-            combine(h)
+            combine(p)
     wait_weight(last)
-    for h in range(heads - 1):
-        send_context(h)
-    project_piece(last)
-    for j in range(R - 1):
-        partial_copy(last, j).wait_recv()
-    combine(heads - 1)
-    send_context(heads - 1)
-
-    for h in range(heads):
+    for u in range(heads - 1):
+        send_context(u)
+    for q in range(last, len(parts)):
+        project_part(q)
+    for q in range(last, len(parts)):
+        for j in range(R - 1):
+            partial_copy(q, j).wait_recv()
+        combine(q - 1)
+        send_context(q - 1)
+
+    for u in range(len(units)):
         for k in range(1, chips):
-            context_copy(h, k - 1).wait_recv()
-            context_forward(h, k).start()
-    for h in range(heads):
+            context_copy(u, k - 1).wait_recv()
+            context_forward(u, k).start()
+    for u in range(len(units)):
         for k in range(chips):
-            context_forward(h, k).wait_recv()
-    out[...] = ctx[...]
+            context_forward(u, k).wait_recv()
+    result = pltpu.make_async_copy(ctx, out, lsem.at[0])
+    result.start()
 
     for c in range(C):
         for j in range(R):
@@ -293,13 +337,15 @@
     for p in range(len(pieces)):
         for k in range(T - 1):
             weight_copy(p, k).wait_send()
-        for j in range(R - 1):
-            partial_copy(p, j).wait_send()
-    for h in range(heads):
+    for q in range(len(parts)):
+        for j in range(R - 1):
+            partial_copy(q, j).wait_send()
+    for u in range(len(units)):
         for k in range(chips - 1):
-            context_copy(h, k).wait_send()
+            context_copy(u, k).wait_send()
         for k in range(chips):
-            context_forward(h, k).wait_send()
+            context_forward(u, k).wait_send()
+    result.wait()
 
 
 def shards(hidden, ln_gain, ln_shift, qkv_weight, qkv_bias, out_weight, out_bias, slope_index):
@@ -315,15 +361,22 @@
     pieces = [(h, 0, wide) for h in range(heads - 1)]
     pieces += [(heads - 1, 0, 2 * size), (heads - 1, 2 * size, size)]
     count = len(pieces)
-    grouped = qkv_weight.reshape(depth, T, heads, wide).transpose(1, 2, 0, 3)
+    parts = [piece + (0, seq) for piece in pieces[:-1]]
+    parts += [pieces[-1] + (0, half), pieces[-1] + (half, half)]
+    units = [(h, 0, seq) for h in range(heads - 1)]
+    units += [(heads - 1, 0, half), (heads - 1, half, half)]
+    chunk = math.gcd(out_weight.shape[0], 128)
     vmem = pl.BlockSpec(memory_space=pltpu.VMEM)
     hbm = pl.BlockSpec(memory_space=pl.ANY)
     dma = pltpu.SemaphoreType.DMA
-    context = pl.pallas_call(
-        functools.partial(fused, R, T, C, pieces),
-        out_shape=jax.ShapeDtypeStruct((seq, T * heads * size), jnp.bfloat16),
-        in_specs=[hbm, vmem, vmem, hbm, vmem, pl.BlockSpec(memory_space=pltpu.SMEM)],
-        out_specs=vmem,
+    context, flat = pl.pallas_call(
+        functools.partial(fused, R, T, C, pieces, parts, units),
+        out_shape=(
+            jax.ShapeDtypeStruct((seq, T * heads * size), jnp.bfloat16),
+            jax.ShapeDtypeStruct((out_weight.shape[0], T * heads * size), jnp.bfloat16),
+        ),
+        in_specs=[hbm, vmem, vmem, hbm, vmem, pl.BlockSpec(memory_space=pltpu.SMEM), hbm],
+        out_specs=(hbm, hbm),
         scratch_shapes=[
             pltpu.VMEM((half, total), jnp.bfloat16),
             pltpu.VMEM((R, half, width), jnp.bfloat16),
@@ -334,6 +387,11 @@
             pltpu.VMEM((seq, seq), jnp.bfloat16),
             pltpu.VMEM((seq, T * heads * size), jnp.bfloat16),
             pltpu.VMEM((heads, width, wide), jnp.bfloat16),
+            pltpu.VMEM((seq, size), jnp.bfloat16),
+            pltpu.VMEM((2, chunk, T * heads, size), jnp.bfloat16),
+            pltpu.VMEM((2, chunk, T * heads * size), jnp.bfloat16),
+            dma((2,)),
+            dma((2,)),
             dma((2 * C,)),
             dma((heads,)),
             dma((count, T - 1)),
@@ -342,12 +400,12 @@
             dma((R - 1, C)),
             dma((R, C)),
             dma((R, C)),
-            dma((count, R - 1)),
-            dma((count, R - 1)),
-            dma((heads, chips - 1)),
-            dma((heads, chips - 1)),
-            dma((heads, chips)),
-            dma((heads, chips)),
+            dma((count + 1, R - 1)),
+            dma((count + 1, R - 1)),
+            dma((len(units), chips - 1)),
+            dma((len(units), chips - 1)),
+            dma((len(units), chips)),
+            dma((len(units), chips)),
         ],
         compiler_params=pltpu.CompilerParams(
             collective_id=0, has_side_effects=True, vmem_limit_bytes=62 * 1024 * 1024
@@ -356,11 +414,11 @@
         hidden,
         ln_gain.reshape(1, total),
         ln_shift.reshape(1, total),
-        grouped,
+        qkv_weight.reshape(depth, T, heads, wide).transpose(1, 2, 0, 3),
         qkv_bias,
         slope_index,
+        out_weight,
     )
-    flat = out_weight.reshape(out_weight.shape[0], -1)
     result = lax.dot_general(
         context, flat, (((1,), (1,)), ((), ())), preferred_element_type=jnp.float32
     )

time: 167 us -> 169 us (1.012)
  no operation moved by 1% of the time
where the time goes in v3:
time: 169 us; the launch traced here: 167 us
  Pallas kernels  152 us (90%)
  matrix products  8.95 us (5%)
  local copies, waits for them, and re-layouts  6.25 us (4%)
    pallas_call x1, Pallas kernels, shards(): pl.pallas_call(functools.partial(fused, R, T, C, pieces, parts, units), o...  152 us
    dot_general x1, matrix products, shards(): lax.dot_general(context, flat, (((1,), (1,)), ((), ())), preferred_elemen...  8.95 us
    unnamed x3, local copies, waits for them, and re-layouts  6.25 us

profile of v3, /device:TPU:0, one launch (start us, length us, event | category | flops | bytes accessed | tf_op | source)
XLA Modules:
  0.0 167.4 jit_solution(17427543169249837716)
XLA Ops:
  0.0 6.3 %copy.9 = bf16[448,16,384]{2,0,1:T(8,128)(2,1)} copy(bf16[448,16,384]{2,1,0:T(8,128)(2,1)} %param.11) | data formatting | bytes 11010048 | tf_op args[3]
  6.3 0.0 copy-start
  6.3 152.1 %shard_map.82 = (bf16[512,2048]{1,0:T(8,128)(2,1)}, bf16[1792,2048]{1,0:T(8,128)(2,1)}) custom-call(bf16[512,14336]{1,0:T(8,128)(2,1)} %hidden.1, f32[1,14336]{1,0:T(1,128)} %bitcast.8, f32[1,14336]{1,0:T(1,128)} %bitcast.9, bf16[8,2,448,384]{3,2,1,0:T(8,128)(2,1)} %bitcast.7, f32[2,384]{1,0:T(2,128)} %bias.1, s32[2]{0:T(128)} %slope_index.1, ...), custom_call_target="tpu_custom_call" | custom-call | tf_op jit(solution)/shard_map/pallas_call | solution.py:372
  158.4 0.0 copy-done
  158.4 9.0 %add_convert_fusion = bf16[512,1792]{1,0:T(8,128)(2,1)} fusion(bf16[512,2048]{1,0:T(8,128)(2,1)} %get-tuple-element.7, bf16[1792,2048]{1,0:T(8,128)(2,1)} %get-tuple-element.8, f32[1792]{0:T(1024)S(1)} %copy-done), kind=kOutput, calls=%fused_computation | convolution fusion | flops 3759931392 | bytes 11279360 | tf_op jit(solution)/shard_map/dot_general | solution.py:422
Async XLA Ops:
  6.3 152.2 %copy-start = (f32[1792]{0:T(1024)S(1)}, f32[1792]{0:T(1024)}, u32[]{:S(2)}) copy-start(f32[1792]{0:T(1024)} %param.14) | copy-start | bytes 21508
